TPU v7x, 32 devices: a whole 2x2x4 slice. The times are simulated.
32 devices in a mesh: groups: 2 (over x), ha: 16 (over z, y, core).
Axes of the slice: x: 2, y: 2, z: 4, core: 2. Of those that a mesh axis runs over, the one named last changes fastest.
Arguments:
- video: bfloat16 [8, 64, 256, 128], P('groups', 'ha'), parts along dimension 0, may hold values from -90 to 90
- cache_video: bfloat16 [4, 64, 256, 128], P('groups', 'ha'), parts along dimension 0, may hold values from -90 to 90
- cache_hidden: bfloat16 [4, 32, 128, 256], P('groups', 'ha'), parts along dimension 0, may hold values from -0.25 to 2
- kernel_down: bfloat16 [3, 3, 3, 128, 256], replicated, may hold values from -0.05103104 to 0.05103104
- gain_down: float32 [256], replicated, may hold values from 0.1 to 1.9
- shift_down: float32 [256], replicated, may hold values from -3 to 3
- kernel_mix: bfloat16 [3, 3, 3, 256, 256], replicated, may hold values from -0.03608439 to 0.03608439
- gain_mix: float32 [256], replicated, may hold values from 0.1 to 1.9
- shift_mix: float32 [256], replicated, may hold values from -3 to 3
Outputs:
- encoded: bfloat16 [8, 32, 128, 256], P('groups', 'ha'), parts along dimension 0
- next_cache: bfloat16 [4, 32, 128, 256], P('groups', 'ha'), parts along dimension 0
There are 2 independent parts, one for each index of `groups`. A program takes and returns all parts, laid end to end along the dimension named above; an argument that names none is the same for every part. Nothing has to cross between parts.
All inputs are finite; a program needn't handle non-finite values.
Results may differ from a plain program's by a relative error of at most 0.0032.
Values may be sent and summed in bfloat16 or wider, within the bound.
A program may use at most 64 MiB of HBM per device.

v0:
```python
import jax
import jax.numpy as jnp
from jax import lax
from jax.sharding import PartitionSpec as P

GROUPS = 32


def shifted(shard, axis, by):
    length = lax.axis_size(axis)
    pairs = [(i, i + by) for i in range(length) if 0 <= i + by < length]
    return lax.ppermute(shard, axis, pairs)


def extended_2(cells, sides, width):
    for axis, dim in sides:
        count = lax.axis_size(axis)
        ends = count - 1
        head = lax.slice_in_dim(cells, 0, width, axis=dim)
        tail = lax.slice_in_dim(cells, cells.shape[dim] - width, cells.shape[dim], axis=dim)
        cells = jnp.concatenate(
            [
                lax.ppermute(tail, axis, [(i, (i + 1) % count) for i in range(ends)]),
                cells,
                lax.ppermute(head, axis, [((i + 1) % count, i) for i in range(ends)]),
            ],
            axis=dim,
        )
    return cells


def convolve(stack, kernel, strides):
    result = lax.conv_general_dilated(
        stack[None],
        kernel,
        strides,
        "VALID",
        dimension_numbers=("NDHWC", "DHWIO", "NDHWC"),
        preferred_element_type=jnp.float32,
    )
    return result[0]


def group_totals(values, per_group):
    return jnp.sum(values, axis=(0, 1, 2)).reshape(-1, per_group).sum(1)


def normalize(values, scales, offsets):
    per_group = values.shape[-1] // GROUPS
    members = values.shape[0] * values.shape[1] * lax.axis_size("ha") * values.shape[2] * per_group
    totals, squares = lax.psum(
        (group_totals(values, per_group), group_totals(values * values, per_group)), "ha"
    )
    center_group = totals / members
    spread_group = squares / members - center_group * center_group
    deviate = values - jnp.repeat(center_group, per_group)
    normed = deviate * jnp.repeat(lax.rsqrt(spread_group + 1e-06), per_group) * scales + offsets
    return jax.nn.silu(normed).astype(jnp.bfloat16)


def local(
    video,
    cache_video,
    cache_hidden,
    kernel_down,
    gain_down,
    shift_down,
    kernel_mix,
    gain_mix,
    shift_mix,
):
    stacked = jnp.concatenate([cache_video, video], axis=0)
    lower_rim = shifted(stacked[:, :1], "ha", -1)
    extended = jnp.concatenate([stacked, lower_rim], axis=1)
    extended = jnp.pad(extended, ((0, 0), (0, 0), (0, 1), (0, 0)))
    first = convolve(extended, kernel_down, (1, 2, 2))
    hidden = normalize(first, gain_down, shift_down)
    padded = extended_2(jnp.concatenate([cache_hidden, hidden], axis=0), (("ha", 1),), 1)
    padded = jnp.pad(padded, ((0, 0), (0, 0), (1, 1), (0, 0)))
    second = convolve(padded, kernel_mix, (1, 1, 1))
    encoded = normalize(second, gain_mix, shift_mix)
    return (encoded, hidden[hidden.shape[0] - 2 :])


def solution(mesh):
    in_specs = (
        P("groups", "ha", None, None),
        P("groups", "ha", None, None),
        P("groups", "ha", None, None),
        P(),
        P(),
        P(),
        P(),
        P(),
        P(),
    )
    out_specs = (P("groups", "ha", None, None), P("groups", "ha", None, None))
    return jax.shard_map(local, mesh=mesh, in_specs=in_specs, out_specs=out_specs, check_vma=False)
```

profile of v0, /device:TPU:0, one launch (start us, length us, event | category | flops | bytes accessed | tf_op | source)
XLA Modules:
  0.0 127.5 jit_solution(16750974581150803377)
XLA Ops:
  0.6 1.2 constant_dynamic-update-slice_fusion.1
  1.9 1.4 %constant_dynamic-update-slice_fusion = bf16[6,4,256,128]{3,2,1,0:T(8,128)(2,1)S(1)} fusion(bf16[6,4,256,128]{3,2,1,0:T(8,128)(2,1)S(1)} %constant_dynamic-update-slice_fusion.1, bf16[4,4,256,128]{3,2,1,0:T(8,128)(2,1)} %param.9), kind=kLoop, calls=%fused_computation.46 | loop fusion | bytes 2097152 | tf_op jit(solution)/shard_map/concatenate | solution.py:72
  3.3 1.3 %collective-permute-start = (bf16[6,1,256,128]{3,2,1,0:T(8,128)(2,1)S(1)}, bf16[6,1,256,128]{3,2,1,0:T(8,128)(2,1)S(1)}, u32[]{:S(2)}, u32[]{:S(2)}) collective-permute-start(bf16[6,1,256,128]{3,2,1,0:T(8,128)(2,1)S(1)} %slice.20), channel_id=1, source_target_pairs={{1,0},{2,1},{3,2},{4,3},{5,4},{6,5},{7,6},{8,7},{9,8},{10,9},{11,1... | collective-permute-start | bytes 1179656 | tf_op jit(solution)/shard_map/ppermute | solution.py:12
  4.6 2.3 %collective-permute-done = bf16[6,1,256,128]{3,2,1,0:T(8,128)(2,1)S(1)} collective-permute-done((bf16[6,1,256,128]{3,2,1,0:T(8,128)(2,1)S(1)}, bf16[6,1,256,128]{3,2,1,0:T(8,128)(2,1)S(1)}, u32[]{:S(2)}, u32[]{:S(2)}) %collective-permute-start) | collective-permute-done | bytes 393248 | tf_op jit(solution)/shard_map/ppermute | solution.py:12
  7.1 1.5 %pad.10 = bf16[6,5,1,272,128]{4,3,1,0,2:T(8,128)(2,1)} pad(bf16[6,5,1,257,128]{4,3,1,0,2:T(8,128)(2,1)S(1)} %fusion.13, bf16[]{:T(256)} %constant.12.clone.1), padding=0_0x0_0x0_0x0_15x0_0 | pad | bytes 4062722 | tf_op jit(solution)/shard_map/broadcast_in_dim | solution.py:34
  8.5 4.5 %reshape.30 = bf16[6,5,1,8,34,128]{5,4,3,1,0,2:T(8,128)(2,1)} reshape(bf16[6,5,1,272,128]{4,3,1,0,2:T(8,128)(2,1)} %pad.10) | data formatting | bytes 4177920 | tf_op jit(solution)/shard_map/conv_general_dilated | solution.py:33
  13.1 2.1 %copy.34 = bf16[6,5,1,8,34,128]{5,3,4,1,0,2:T(8,128)(2,1)S(1)} copy(bf16[6,5,1,8,34,128]{5,4,3,1,0,2:T(8,128)(2,1)} %reshape.30) | data formatting | bytes 4177920 | tf_op jit(solution)/shard_map/conv_general_dilated | solution.py:33
  15.3 3.8 %select_reduce_fusion.1 = (f32[256]{0:T(256)}, f32[4,2,8,17,256]{4,2,3,1,0:T(8,128)}) fusion(pred[8,17]{0,1:T(8,128)(4,1)S(1)} %copy-done.5, bf16[3,3,3,128,256]{4,3,2,1,0:T(8,128)(2,1)S(1)} %copy-done.4, bf16[6,5,1,7,2,128]{5,3,4,1,0,2:T(8,128)(2,1)S(1)} %slice.21, bf16[6,5,1,8,34,128]{5,3,4,1,0,2:T(8,128)(2,1)S(1)} %copy.34), kind=kOutput, calls=%fused_computation.33 | convolution fusion | flops 1932656384 | bytes 5081224 | tf_op jit(solution)/shard_map/conv_general_dilated | solution.py:33
  19.1 0.8 reshape.24
  19.8 1.8 %copy.35 = f32[4,2,8,17,256]{4,1,3,2,0:T(2,128)S(1)} copy(f32[4,2,8,17,256]{4,2,3,1,0:T(8,128)} %get-tuple-element.17) | data formatting | bytes 2228224 | tf_op jit(solution)/shard_map/conv_general_dilated | solution.py:33
  22.0 1.0 copy-done.1
  23.0 0.7 multiply_reduce_fusion.1
  23.7 1.4 %reshape.25 = f32[32,8]{1,0:T(8,128)} reshape(f32[256]{0:T(256)} %multiply_reduce_fusion.1) | data formatting | bytes 2048 | tf_op jit(solution)/shard_map/reshape | solution.py:45
  25.7 0.8 reduce_sum.75
  26.6 36.5 %all-reduce.3 = (f32[32]{0:T(128)S(1)}, f32[32]{0:T(128)S(1)}) all-reduce(f32[32]{0:T(128)S(1)} %reduce_sum.75, f32[32]{0:T(128)} %reduce_sum.73), channel_id=1, replica_groups=mesh['groups'=2,'ha'=16] {'ha'}, use_global_device_ids=true, to_apply=%region_5.6 | all-reduce | flops 64 | bytes 512 | tf_op jit(solution)/shard_map/psum | solution.py:51
  64.3 0.7 broadcast_in_dim.24
  65.7 1.6 %multiply_convert_fusion.1 = bf16[4,2,128,256]{3,2,1,0:T(8,128)(2,1)S(1)} fusion(f32[4,2,1,128,256]{4,1,3,0,2:T(2,128)} %copy-done.1, f32[256]{0:T(256)} %param.14, f32[256]{0:T(256)} %param.13, f32[256]{0:T(256)} %mul.57, f32[256]{0:T(256)} %sub.26), kind=kLoop, calls=%fused_computation.39 | loop fusion | flops 2359296 | bytes 1576960 | tf_op jit(solution)/shard_map/convert_element_type | solution.py:58
  67.3 1.0 fusion.33
  68.4 1.3 %collective-permute-start.1 = (bf16[6,1,128,256]{3,2,1,0:T(8,128)(2,1)S(1)}, bf16[6,1,128,256]{3,2,1,0:T(8,128)(2,1)S(1)}, u32[]{:S(2)}, u32[]{:S(2)}) collective-permute-start(bf16[6,1,128,256]{3,2,1,0:T(8,128)(2,1)S(1)} %get-tuple-element.10), channel_id=1, source_target_pairs={{0,1},{1,2},{2,3},{3,4},{4,5},{5,6},{6,7},{7,8},{8,9},{9,10},{10,1... | collective-permute-start | bytes 1179656 | tf_op jit(solution)/shard_map/ppermute | solution.py:23
  69.7 1.5 %collective-permute-start.2 = (bf16[6,1,128,256]{3,2,1,0:T(8,128)(2,1)S(1)}, bf16[6,1,128,256]{3,2,1,0:T(8,128)(2,1)S(1)}, u32[]{:S(2)}, u32[]{:S(2)}) collective-permute-start(bf16[6,1,128,256]{3,2,1,0:T(8,128)(2,1)S(1)} %get-tuple-element.11), channel_id=1, source_target_pairs={{1,0},{2,1},{3,2},{4,3},{5,4},{6,5},{7,6},{8,7},{9,8},{10,9},{11,1... | collective-permute-start | bytes 1179656 | tf_op jit(solution)/shard_map/ppermute | solution.py:25
  71.2 0.7 slice.27
  71.9 1.4 %collective-permute-done.2 = bf16[6,1,128,256]{3,2,1,0:T(8,128)(2,1)S(1)} collective-permute-done((bf16[6,1,128,256]{3,2,1,0:T(8,128)(2,1)S(1)}, bf16[6,1,128,256]{3,2,1,0:T(8,128)(2,1)S(1)}, u32[]{:S(2)}, u32[]{:S(2)}) %collective-permute-start.2) | collective-permute-done | bytes 393248 | tf_op jit(solution)/shard_map/ppermute | solution.py:25
  73.3 0.9 fusion.21
  76.1 5.6 %select_reduce_fusion = (f32[256]{0:T(256)}, f32[4,2,8,17,256]{4,2,3,1,0:T(8,128)}) fusion(pred[8,17]{0,1:T(8,128)(4,1)S(1)} %copy-done.6, bf16[3,3,3,256,256]{4,3,2,1,0:T(8,128)(2,1)S(1)} %copy-done, bf16[6,4,1,7,2,256]{5,3,4,1,0,2:T(8,128)(2,1)S(1)} %slice.25, bf16[6,4,1,8,17,256]{5,3,4,1,0,2:T(8,128)(2,1)S(1)} %copy.39), kind=kOutput, calls=%fused_computation.32 | convolution fusion | flops 3856809728 | bytes 6497416 | tf_op jit(solution)/shard_map/conv_general_dilated | solution.py:33
  81.8 0.8 reshape.26
  83.1 1.8 %copy.40 = f32[4,2,8,17,256]{4,1,3,2,0:T(2,128)S(1)} copy(f32[4,2,8,17,256]{4,2,3,1,0:T(8,128)} %get-tuple-element.19) | data formatting | bytes 2228224 | tf_op jit(solution)/shard_map/conv_general_dilated | solution.py:33
  85.3 1.0 copy-done.2
  86.3 0.7 multiply_reduce_fusion
  87.0 0.8 reshape.27
  88.4 34.0 %all-reduce.2 = (f32[32]{0:T(128)S(1)}, f32[32]{0:T(128)S(1)}) all-reduce(f32[32]{0:T(128)} %reduce_sum.79, f32[32]{0:T(128)} %reduce_sum.77), channel_id=1, replica_groups=mesh['groups'=2,'ha'=16] {'ha'}, use_global_device_ids=true, to_apply=%region_11.12 | all-reduce | flops 64 | bytes 512 | tf_op jit(solution)/shard_map/psum | solution.py:51
  123.7 0.7 broadcast_in_dim.27
  125.1 2.4 %multiply_convert_fusion = bf16[4,2,128,256]{3,2,1,0:T(8,128)(2,1)} fusion(f32[4,2,1,128,256]{4,1,3,0,2:T(2,128)} %copy-done.2, f32[256]{0:T(256)} %param.17, f32[256]{0:T(256)} %param.16, f32[256]{0:T(256)} %mul.65, f32[256]{0:T(256)} %sub.30), kind=kLoop, calls=%fused_computation.37 | loop fusion | flops 2359296 | bytes 1576960 | tf_op jit(solution)/shard_map/convert_element_type | solution.py:58
  (33 shorter events, 8.7 us)
Async XLA Ops:
  0.6 75.1 %copy-start = (bf16[3,3,3,256,256]{4,3,2,1,0:T(8,128)(2,1)S(1)}, bf16[3,3,3,256,256]{4,3,2,1,0:T(8,128)(2,1)}, u32[]{:S(2)}) copy-start(bf16[3,3,3,256,256]{4,3,2,1,0:T(8,128)(2,1)} %param.15) | copy-start | bytes 10616836
  3.3 3.6 %collective-permute-start = (bf16[6,1,256,128]{3,2,1,0:T(8,128)(2,1)S(1)}, bf16[6,1,256,128]{3,2,1,0:T(8,128)(2,1)S(1)}, u32[]{:S(2)}, u32[]{:S(2)}) collective-permute-start(bf16[6,1,256,128]{3,2,1,0:T(8,128)(2,1)S(1)} %slice.20), channel_id=1, source_target_pairs={{1,0},{2,1},{3,2},{4,3},{5,4},{6,5},{7,6},{8,7},{9,8},{10,9},{11,1... | collective-permute-start | bytes 1179656 | tf_op jit(solution)/shard_map/ppermute | solution.py:12
  13.1 2.2 %copy-start.4 = (bf16[3,3,3,128,256]{4,3,2,1,0:T(8,128)(2,1)S(1)}, bf16[3,3,3,128,256]{4,3,2,1,0:T(8,128)(2,1)}, u32[]{:S(2)}) copy-start(bf16[3,3,3,128,256]{4,3,2,1,0:T(8,128)(2,1)} %param.12) | copy-start | bytes 5308420
  13.1 2.2 %copy-start.5 = (pred[8,17]{0,1:T(8,128)(4,1)S(1)}, pred[8,17]{0,1:T(8,128)(4,1)}, u32[]{:S(2)}) copy-start(pred[8,17]{0,1:T(8,128)(4,1)} %constant.34) | copy-start | bytes 412
  22.0 1.0 copy-start.1
  65.7 7.6 %copy-start.3 = (bf16[2,2,128,256]{3,2,1,0:T(8,128)(2,1)S(1)}, bf16[2,2,128,256]{3,2,1,0:T(8,128)(2,1)}, u32[]{:S(2)}) copy-start(bf16[2,2,128,256]{3,2,1,0:T(8,128)(2,1)} %param.11) | copy-start | bytes 786436
  68.4 3.5 %collective-permute-start.1 = (bf16[6,1,128,256]{3,2,1,0:T(8,128)(2,1)S(1)}, bf16[6,1,128,256]{3,2,1,0:T(8,128)(2,1)S(1)}, u32[]{:S(2)}, u32[]{:S(2)}) collective-permute-start(bf16[6,1,128,256]{3,2,1,0:T(8,128)(2,1)S(1)} %get-tuple-element.10), channel_id=1, source_target_pairs={{0,1},{1,2},{2,3},{3,4},{4,5},{5,6},{6,7},{7,8},{8,9},{9,10},{10,1... | collective-permute-start | bytes 1179656 | tf_op jit(solution)/shard_map/ppermute | solution.py:23
  69.7 3.6 %collective-permute-start.2 = (bf16[6,1,128,256]{3,2,1,0:T(8,128)(2,1)S(1)}, bf16[6,1,128,256]{3,2,1,0:T(8,128)(2,1)S(1)}, u32[]{:S(2)}, u32[]{:S(2)}) collective-permute-start(bf16[6,1,128,256]{3,2,1,0:T(8,128)(2,1)S(1)} %get-tuple-element.11), channel_id=1, source_target_pairs={{1,0},{2,1},{3,2},{4,3},{5,4},{6,5},{7,6},{8,7},{9,8},{10,9},{11,1... | collective-permute-start | bytes 1179656 | tf_op jit(solution)/shard_map/ppermute | solution.py:25
  75.5 0.7 copy-start.6
  85.3 1.0 copy-start.2
where the time goes:
time: 128 us; the launch traced here: 127 us
  blocking collectives  70.5 us (55%)
  local copies, waits for them, and re-layouts  27.7 us (22%)
  other arithmetic  11.3 us (9%)
  matrix products  9.39 us (7%)
  starting transfers between devices  4.08 us (3%)
  waiting for transfers between devices  3.73 us (3%)
    psum x2, blocking collectives, normalize(): lax.psum((group_totals(values, per_group), group_totals(values * values,...  70.5 us
    conv_general_dilated x9, local copies, waits for them, and re-layouts, convolve(): lax.conv_general_dilated(stack[None], kernel, strides, 'VALID', dimension...  11.3 us
    conv_general_dilated x2, matrix products, convolve(): lax.conv_general_dilated(stack[None], kernel, strides, 'VALID', dimension...  9.39 us
    unnamed x16, local copies, waits for them, and re-layouts  4.29 us
    reduce_sum x6, other arithmetic, group_totals(): return jnp.sum(values, axis=(0, 1, 2)).reshape(-1, per_group).sum(1)  4.14 us
    convert_element_type x2, other arithmetic, normalize(): return jax.nn.silu(normed).astype(jnp.bfloat16)  4.01 us
    reshape x4, local copies, waits for them, and re-layouts, group_totals(): return jnp.sum(values, axis=(0, 1, 2)).reshape(-1, per_group).sum(1)  3.64 us
  transfers between devices with their start and end apart: 3, of which 2 were waited for; matrix products, arithmetic and copies ran while one was open for 1% of the time, Pallas kernels for 0%

commit v1 on v0

v1 whole, which is shorter than its diff:
```python
import functools

import jax
import jax.numpy as jnp
from jax import lax
from jax.experimental import pallas as pl
from jax.experimental.pallas import tpu as pltpu
from jax.sharding import PartitionSpec as P

GROUPS = 32
MESH = pl.DeviceIdType.MESH
F32 = jnp.float32
BF16 = jnp.bfloat16


def kernel(
    n,
    video,
    cache_video,
    cache_hidden,
    w_down,
    gain_down,
    shift_down,
    w_mix,
    gain_mix,
    shift_mix,
    encoded,
    next_cache,
    vid,
    rim,
    raw,
    x1,
    w1,
    w2,
    x2,
    acc1,
    acc2,
    right,
    left,
    stats,
    enc,
    load_sem,
    rim_send,
    rim_recv,
    hid_send,
    hid_recv,
    stat_send,
    stat_recv,
    out_sem,
):
    frames, rows, width, c_in = video.shape
    past = cache_video.shape[0]
    total = frames + past
    out_rows, cols, c_out = cache_hidden.shape[1:]
    m = frames * cols
    me = lax.axis_index("ha")
    has_up = me > 0
    has_down = me < n - 1

    barrier = pltpu.get_barrier_semaphore()

    @pl.loop(1, n)
    def _(k):
        pl.semaphore_signal(barrier, inc=1, device_id={"ha": lax.rem(me + k, n)}, device_id_type=MESH)

    loads = []
    for t in range(total):
        src = cache_video.at[t] if t < past else video.at[t - past]
        loads.append((src, vid.at[t]))
    for a in range(3):
        loads.append((w_down.at[pl.ds(3 * a, 3)], w1.at[pl.ds(3 * a, 3)]))
    for a in range(3):
        loads.append((w_mix.at[pl.ds(3 * a, 3)], w2.at[pl.ds(3 * a, 3)]))
    for t in range(past):
        for r in range(out_rows):
            loads.append((cache_hidden.at[t, r], x2.at[1 + r, pl.ds(t * cols, cols)]))
    copies = [pltpu.make_async_copy(s, d, load_sem.at[i]) for i, (s, d) in enumerate(loads)]
    for copy in copies:
        copy.start()

    right[:, :, pl.ds(cols, 8), :] = jnp.zeros(right.shape[:2] + (8, c_out), F32)
    left[:, :, pl.ds(0, 8), :] = jnp.zeros(left.shape[:2] + (8, c_out), F32)

    def rim_copy(t):
        src = cache_video.at[t, 0] if t < past else video.at[t - past, 0]
        return pltpu.make_async_remote_copy(
            src_ref=src, dst_ref=rim.at[t], send_sem=rim_send.at[t], recv_sem=rim_recv.at[t],
            device_id={"ha": me - 1}, device_id_type=MESH,
        )

    def hid_copy(up, t):
        span = pl.ds(t * cols, cols)
        if t < past:
            src = cache_hidden.at[t, 0 if up else out_rows - 1]
        else:
            src = x2.at[1 if up else out_rows, span]
        side = 0 if up else 1
        return pltpu.make_async_remote_copy(
            src_ref=src, dst_ref=x2.at[out_rows + 1 if up else 0, span],
            send_sem=hid_send.at[side, t], recv_sem=hid_recv.at[side, t],
            device_id={"ha": me - 1 if up else me + 1}, device_id_type=MESH,
        )

    pl.semaphore_wait(barrier, n - 1)

    @pl.when(has_up)
    def _():
        for t in range(total):
            rim_copy(t).start()
        for t in range(past):
            hid_copy(True, t).start()

    @pl.when(has_down)
    def _():
        for t in range(past):
            hid_copy(False, t).start()

    @pl.when(jnp.logical_not(has_up))
    def _():
        x2[0] = jnp.zeros(x2.shape[1:], BF16)

    @pl.when(jnp.logical_not(has_down))
    def _():
        x2[out_rows + 1] = jnp.zeros(x2.shape[1:], BF16)
        x1[rows] = jnp.zeros(x1.shape[1:], BF16)

    def split(src, slot, r, t):
        raw[slot] = src.astype(F32)
        x1[r, pl.ds(t * cols, cols), 0:c_in] = raw[slot, pl.ds(0, cols, stride=2), :].astype(BF16)
        x1[r, pl.ds(t * cols, cols), c_in:] = raw[slot, pl.ds(1, cols, stride=2), :].astype(BF16)

    for t in range(total):
        copies[t].wait()
        for r in range(rows):
            split(vid[t, r], r, r, t)
    for a in range(3):
        copies[total + a].wait()

    def taps(x, lanes, w, depth, pairs):
        lhs = jnp.concatenate([x[r, pl.ds(a * cols, m), lanes] for a, r, b in pairs], axis=1)
        rhs = jnp.concatenate([w[3 * a + b, depth, :] for a, r, b in pairs], axis=0)
        return jnp.dot(lhs, rhs, preferred_element_type=F32)

    both, even = slice(0, 2 * c_in), slice(0, c_in)
    near, far = slice(0, 2 * c_in), slice(2 * c_in, 3 * c_in)

    def as_frames(v):
        return v.reshape(frames, cols, c_out)

    for i in range(out_rows):
        pairs = [(a, 2 * i + b, b) for b in range(3) if 2 * i + b < rows for a in range(3)]
        acc1[i] = taps(x1, both, w1, near, pairs)
        right[i, :, pl.ds(0, cols), :] = as_frames(taps(x1, even, w1, far, pairs))

    @pl.when(has_down)
    def _():
        for t in range(total):
            rim_copy(t).wait_recv()
            split(rim[t], t % rows, rows, t)

    pairs = [(a, rows, 2) for a in range(3)]
    last = out_rows - 1
    acc1[last] += taps(x1, both, w1, near, pairs)
    right[last, :, pl.ds(0, cols), :] += as_frames(taps(x1, even, w1, far, pairs))

    def sums(parts, s, q, v):
        v8 = v.reshape(cols // 8, 8, c_out)
        return s + jnp.sum(v8, axis=0), q + jnp.sum(v8 * v8, axis=0)

    def stat_copy(phase, owner, peer, k):
        return pltpu.make_async_remote_copy(
            src_ref=stats.at[phase, me], dst_ref=stats.at[phase, owner],
            send_sem=stat_send.at[phase, k], recv_sem=stat_recv.at[phase, owner],
            device_id={"ha": peer}, device_id_type=MESH,
        )

    def send_stats(phase, s, q):
        stats[phase, me] = jnp.concatenate(
            [jnp.sum(s, axis=0, keepdims=True), jnp.sum(q, axis=0, keepdims=True)], axis=0
        )

        @pl.loop(1, n)
        def _(k):
            stat_copy(phase, me, lax.rem(me + k, n), k).start()

    per_group = c_out // GROUPS
    members = float(frames * out_rows * n * cols * per_group)

    def wait_stats(phase):
        @pl.loop(1, n)
        def _(k):
            peer = lax.rem(me + k, n)
            stat_copy(phase, peer, peer, k).wait_recv()

        both_sums = jnp.sum(stats[phase], axis=0)
        lane = lax.broadcasted_iota(jnp.int32, (8, c_out), 1)

        def grouped(v):
            v = jnp.broadcast_to(v, (8, c_out))
            step = 1
            while step < per_group:
                below = pltpu.roll(v, step, 1)
                above = pltpu.roll(v, c_out - step, 1)
                v = v + jnp.where((lane & step) == 0, above, below)
                step *= 2
            return v[0:1]

        center = grouped(both_sums[0:1]) / members
        spread = jnp.maximum(grouped(both_sums[1:2]) / members - center * center, 0.0)
        return center, lax.rsqrt(spread + 1e-06)

    def activate(v, center, scale, shift):
        v = (v - center) * scale + shift
        return (v / (1.0 + jnp.exp(-v))).astype(BF16)

    s = q = jnp.zeros((8, c_out), F32)
    for i in range(out_rows):
        for t in range(frames):
            span = pl.ds(t * cols, cols)
            v = acc1[i, span, :] + right[i, t, pl.ds(1, cols), :]
            acc1[i, span, :] = v
            s, q = sums(None, s, q, v)
    send_stats(0, s, q)

    for i in range(total + 3, len(copies)):
        copies[i].wait()

    center, inverse = wait_stats(0)
    scale = inverse * gain_down[...]
    shift = shift_down[...]
    for t in range(frames):
        for i in range(out_rows):
            x2[1 + i, pl.ds((past + t) * cols, cols), :] = activate(
                acc1[i, pl.ds(t * cols, cols), :], center, scale, shift
            )

        @pl.when(has_up)
        def _():
            hid_copy(True, past + t).start()

        @pl.when(has_down)
        def _():
            hid_copy(False, past + t).start()

    outs = []
    for t in range(past):
        for r in range(out_rows):
            src = x2.at[1 + r, pl.ds((total - past + t) * cols, cols)]
            outs.append(pltpu.make_async_copy(src, next_cache.at[t, r], out_sem.at[len(outs)]))
            outs[-1].start()

    everything = slice(0, c_out)

    def mix(i, c, pairs):
        return taps(x2, everything, w2, pl.ds(c * c_out, c_out), pairs)

    for i in range(out_rows):
        pairs = [(a, i + b, b) for b in range(3) if 1 <= i + b <= out_rows for a in range(3)]
        left[i, :, pl.ds(8, cols), :] = as_frames(mix(i, 0, pairs))
        acc2[i] = mix(i, 1, pairs)
        right[i, :, pl.ds(0, cols), :] = as_frames(mix(i, 2, pairs))

    @pl.when(has_up)
    def _():
        for t in range(total):
            hid_copy(False, t).wait_recv()

    @pl.when(has_down)
    def _():
        for t in range(total):
            hid_copy(True, t).wait_recv()

    s = q = jnp.zeros((8, c_out), F32)
    for i in range(out_rows):
        pairs = [(a, i + b, b) for b in range(3) if not 1 <= i + b <= out_rows for a in range(3)]
        if pairs:
            left[i, :, pl.ds(8, cols), :] += as_frames(mix(i, 0, pairs))
            acc2[i] += mix(i, 1, pairs)
            right[i, :, pl.ds(0, cols), :] += as_frames(mix(i, 2, pairs))
        for t in range(frames):
            span = pl.ds(t * cols, cols)
            v = acc2[i, span, :] + left[i, t, pl.ds(7, cols), :] + right[i, t, pl.ds(1, cols), :]
            acc2[i, span, :] = v
            s, q = sums(None, s, q, v)
    send_stats(1, s, q)

    center, inverse = wait_stats(1)
    scale = inverse * gain_mix[...]
    shift = shift_mix[...]
    for t in range(frames):
        for i in range(out_rows):
            enc[t, i] = activate(acc2[i, pl.ds(t * cols, cols), :], center, scale, shift)
        outs.append(pltpu.make_async_copy(enc.at[t], encoded.at[t], out_sem.at[len(outs)]))
        outs[-1].start()

    @pl.when(has_up)
    def _():
        for t in range(total):
            rim_copy(t).wait_send()
            hid_copy(True, t).wait_send()

    @pl.when(has_down)
    def _():
        for t in range(total):
            hid_copy(False, t).wait_send()

    for phase in range(2):

        @pl.loop(1, n)
        def _(k):
            stat_copy(phase, me, lax.rem(me + k, n), k).wait_send()

    for copy in outs:
        copy.wait()


def local(n, video, cache_video, cache_hidden, kernel_down, gain_down, shift_down, kernel_mix, gain_mix, shift_mix):
    frames, rows, width, c_in = video.shape
    past, out_rows, cols, c_out = cache_hidden.shape
    total = frames + past
    hbm = pl.BlockSpec(memory_space=pl.ANY)
    vmem = pl.BlockSpec(memory_space=pltpu.VMEM)
    row = lambda v: v.reshape(1, c_out)
    return pl.pallas_call(
        functools.partial(kernel, n),
        out_shape=(
            jax.ShapeDtypeStruct((frames, out_rows, cols, c_out), BF16),
            jax.ShapeDtypeStruct((past, out_rows, cols, c_out), BF16),
        ),
        in_specs=[hbm, hbm, hbm, hbm, vmem, vmem, hbm, vmem, vmem],
        out_specs=(hbm, hbm),
        scratch_shapes=[
            pltpu.VMEM((total, rows, width, c_in), BF16),
            pltpu.VMEM((total, width, c_in), BF16),
            pltpu.VMEM((rows, width, c_in), F32),
            pltpu.VMEM((rows + 1, total * cols, 2 * c_in), BF16),
            pltpu.VMEM((9, 3 * c_in, c_out), BF16),
            pltpu.VMEM((9, 3 * c_out, c_out), BF16),
            pltpu.VMEM((out_rows + 2, total * cols, c_out), BF16),
            pltpu.VMEM((out_rows, frames * cols, c_out), F32),
            pltpu.VMEM((out_rows, frames * cols, c_out), F32),
            pltpu.VMEM((out_rows, frames, cols + 8, c_out), F32),
            pltpu.VMEM((out_rows, frames, cols + 8, c_out), F32),
            pltpu.VMEM((2, n, 2, c_out), F32),
            pltpu.VMEM((frames, out_rows, cols, c_out), BF16),
            pltpu.SemaphoreType.DMA((total + 6 + past * out_rows,)),
            pltpu.SemaphoreType.DMA((total,)),
            pltpu.SemaphoreType.DMA((total,)),
            pltpu.SemaphoreType.DMA((2, total)),
            pltpu.SemaphoreType.DMA((2, total)),
            pltpu.SemaphoreType.DMA((2, n)),
            pltpu.SemaphoreType.DMA((2, n)),
            pltpu.SemaphoreType.DMA((past * out_rows + frames,)),
        ],
        compiler_params=pltpu.CompilerParams(
            collective_id=0, has_side_effects=True, vmem_limit_bytes=48 * 1024 * 1024
        ),
    )(
        video,
        cache_video,
        cache_hidden,
        kernel_down.reshape(9, 3 * c_in, c_out),
        row(gain_down),
        row(shift_down),
        kernel_mix.reshape(9, 3 * c_out, c_out),
        row(gain_mix),
        row(shift_mix),
    )


def solution(mesh):
    split = P("groups", "ha", None, None)
    return jax.shard_map(
        functools.partial(local, mesh.shape["ha"]),
        mesh=mesh,
        in_specs=(split, split, split) + (P(),) * 6,
        out_specs=(split, split),
        check_vma=False,
    )
```

time: 128 us -> 41.9 us (0.33)
  blocking collectives: 70.5 us -> 0 us
  Pallas kernels: 0 us -> 32 us
  local copies, waits for them, and re-layouts: 27.7 us -> 8.9 us
  other arithmetic: 11.3 us -> 0 us
  matrix products: 9.39 us -> 0 us
  starting transfers between devices: 4.08 us -> 0 us
  waiting for transfers between devices: 3.73 us -> 0 us
    psum x2 -> x0, blocking collectives: 70.5 us -> none  [normalize(): lax.psum((group_totals(values, per_group), group_totals(values * values,...]
    pallas_call x0 -> x1, Pallas kernels: none -> 32 us  [local(): pl.pallas_call(functools.partial(kernel, n), out_shape=(jax.ShapeDtypeStr...]
    conv_general_dilated x9 -> x0, local copies, waits for them, and re-layouts: 11.3 us -> none  [convolve(): lax.conv_general_dilated(stack[None], kernel, strides, 'VALID', dimension...]
    conv_general_dilated x2 -> x0, matrix products: 9.39 us -> none  [convolve(): lax.conv_general_dilated(stack[None], kernel, strides, 'VALID', dimension...]
    unnamed x16 -> x18, local copies, waits for them, and re-layouts: 4.29 us -> 8.9 us
    reduce_sum x6 -> x0, other arithmetic: 4.14 us -> none  [group_totals(): return jnp.sum(values, axis=(0, 1, 2)).reshape(-1, per_group).sum(1)]
    ppermute x3 -> x0, starting transfers between devices: 4.08 us -> none  [the longest x1 1.47 us: extended_2(): lax.ppermute(head, axis, [((i + 1) % count, i) for i in range(ends)])]
    convert_element_type x2 -> x0, other arithmetic: 4.01 us -> none  [normalize(): return jax.nn.silu(normed).astype(jnp.bfloat16)]
  transfers between devices with their start and end apart: 3 -> 0, of which waited for: 2 -> 0; matrix products, arithmetic and copies ran while one was open for 1% -> 0% of each run, Pallas kernels for 0% -> 0%
where the time goes in v1:
time: 41.9 us; the launch traced here: 41.6 us
  Pallas kernels  32 us (76%)
  local copies, waits for them, and re-layouts  8.9 us (21%)
  between operations  0.66 us (2%)
    pallas_call x1, Pallas kernels, local(): pl.pallas_call(functools.partial(kernel, n), out_shape=(jax.ShapeDtypeStr...  32 us
    unnamed x18, local copies, waits for them, and re-layouts  8.9 us

profile of v1, /device:TPU:0, one launch (start us, length us, event | category | flops | bytes accessed | tf_op | source)
XLA Modules:
  0.0 41.6 jit_solution(5346633401057816741)
XLA Ops:
  0.6 0.0 copy-start
  0.6 1.5 %copy-done = bf16[3,3,3,128,256]{4,3,2,1,0:T(8,128)(2,1)S(1)} copy-done((bf16[3,3,3,128,256]{4,3,2,1,0:T(8,128)(2,1)S(1)}, bf16[3,3,3,128,256]{4,3,2,1,0:T(8,128)(2,1)}, u32[]{:S(2)}) %copy-start) | copy-done | bytes 1769496
  2.1 0.0 copy-start.1
  2.1 1.2 %copy-done.1 = bf16[4,4,256,128]{3,2,1,0:T(8,128)(2,1)S(1)} copy-done((bf16[4,4,256,128]{3,2,1,0:T(8,128)(2,1)S(1)}, bf16[4,4,256,128]{3,2,1,0:T(8,128)(2,1)}, u32[]{:S(2)}) %copy-start.1) | copy-done | bytes 1048600
  3.3 0.0 copy-start.2
  3.3 1.0 %copy-done.2 = bf16[2,4,256,128]{3,2,1,0:T(8,128)(2,1)S(1)} copy-done((bf16[2,4,256,128]{3,2,1,0:T(8,128)(2,1)S(1)}, bf16[2,4,256,128]{3,2,1,0:T(8,128)(2,1)}, u32[]{:S(2)}) %copy-start.2) | copy-done | bytes 524312
  4.4 0.0 copy-start.3
  4.4 0.9 %copy-done.3 = bf16[2,2,128,256]{3,2,1,0:T(8,128)(2,1)S(1)} copy-done((bf16[2,2,128,256]{3,2,1,0:T(8,128)(2,1)S(1)}, bf16[2,2,128,256]{3,2,1,0:T(8,128)(2,1)}, u32[]{:S(2)}) %copy-start.3) | copy-done | bytes 262168
  5.3 0.0 copy-start.4
  5.3 0.7 %copy-done.4 = f32[256]{0:T(256)S(1)} copy-done((f32[256]{0:T(256)S(1)}, f32[256]{0:T(256)}, u32[]{:S(2)}) %copy-start.4) | copy-done | bytes 1048
  6.0 0.0 copy-start.5
  6.0 0.7 %copy-done.5 = f32[256]{0:T(256)S(1)} copy-done((f32[256]{0:T(256)S(1)}, f32[256]{0:T(256)}, u32[]{:S(2)}) %copy-start.5) | copy-done | bytes 1048
  6.7 0.0 copy-start.6
  6.7 0.7 %copy-done.6 = f32[256]{0:T(256)S(1)} copy-done((f32[256]{0:T(256)S(1)}, f32[256]{0:T(256)}, u32[]{:S(2)}) %copy-start.6) | copy-done | bytes 1048
  7.4 0.0 copy-start.7
  7.4 0.7 %copy-done.7 = f32[256]{0:T(256)S(1)} copy-done((f32[256]{0:T(256)S(1)}, f32[256]{0:T(256)}, u32[]{:S(2)}) %copy-start.7) | copy-done | bytes 1048
  8.0 32.0 %shard_map.104 = (bf16[4,2,128,256]{3,2,1,0:T(8,128)(2,1)S(1)}, bf16[2,2,128,256]{3,2,1,0:T(8,128)(2,1)S(1)}) custom-call(bf16[4,4,256,128]{3,2,1,0:T(8,128)(2,1)S(1)} %copy-done.1, bf16[2,4,256,128]{3,2,1,0:T(8,128)(2,1)S(1)} %copy-done.2, bf16[2,2,128,256]{3,2,1,0:T(8,128)(2,1)S(1)} %copy-done.3, bf16[9,384,256]{2,1,0:T(8,128)(2,1)S(1)} %bitcast.6, ...), custom_call_target="tpu_custom_call" | custom-call | tf_op jit(solution)/shard_map/pallas_call | solution.py:324
  40.1 0.8 %copy.13 = bf16[4,2,128,256]{3,2,1,0:T(8,128)(2,1)} copy(bf16[4,2,128,256]{3,2,1,0:T(8,128)(2,1)S(1)} %get-tuple-element.4) | data formatting | bytes 1048576
  40.9 0.7 %copy.14 = bf16[2,2,128,256]{3,2,1,0:T(8,128)(2,1)} copy(bf16[2,2,128,256]{3,2,1,0:T(8,128)(2,1)S(1)} %get-tuple-element.5) | data formatting | bytes 524288
Async XLA Ops:
  0.6 1.5 %copy-start = (bf16[3,3,3,128,256]{4,3,2,1,0:T(8,128)(2,1)S(1)}, bf16[3,3,3,128,256]{4,3,2,1,0:T(8,128)(2,1)}, u32[]{:S(2)}) copy-start(bf16[3,3,3,128,256]{4,3,2,1,0:T(8,128)(2,1)} %param.12) | copy-start | bytes 5308420
  2.1 1.2 %copy-start.1 = (bf16[4,4,256,128]{3,2,1,0:T(8,128)(2,1)S(1)}, bf16[4,4,256,128]{3,2,1,0:T(8,128)(2,1)}, u32[]{:S(2)}) copy-start(bf16[4,4,256,128]{3,2,1,0:T(8,128)(2,1)} %video.1) | copy-start | bytes 3145732
  3.3 1.0 %copy-start.2 = (bf16[2,4,256,128]{3,2,1,0:T(8,128)(2,1)S(1)}, bf16[2,4,256,128]{3,2,1,0:T(8,128)(2,1)}, u32[]{:S(2)}) copy-start(bf16[2,4,256,128]{3,2,1,0:T(8,128)(2,1)} %cache_video.1) | copy-start | bytes 1572868
  4.4 0.9 %copy-start.3 = (bf16[2,2,128,256]{3,2,1,0:T(8,128)(2,1)S(1)}, bf16[2,2,128,256]{3,2,1,0:T(8,128)(2,1)}, u32[]{:S(2)}) copy-start(bf16[2,2,128,256]{3,2,1,0:T(8,128)(2,1)} %cache_hidden.1) | copy-start | bytes 786436
  5.3 0.7 %copy-start.4 = (f32[256]{0:T(256)S(1)}, f32[256]{0:T(256)}, u32[]{:S(2)}) copy-start(f32[256]{0:T(256)} %param.13) | copy-start | bytes 3076
  6.0 0.7 %copy-start.5 = (f32[256]{0:T(256)S(1)}, f32[256]{0:T(256)}, u32[]{:S(2)}) copy-start(f32[256]{0:T(256)} %param.14) | copy-start | bytes 3076
  6.7 0.7 %copy-start.6 = (f32[256]{0:T(256)S(1)}, f32[256]{0:T(256)}, u32[]{:S(2)}) copy-start(f32[256]{0:T(256)} %param.16) | copy-start | bytes 3076
  7.4 0.7 %copy-start.7 = (f32[256]{0:T(256)S(1)}, f32[256]{0:T(256)}, u32[]{:S(2)}) copy-start(f32[256]{0:T(256)} %param.17) | copy-start | bytes 3076

commit v2 on v1

--- a/solution.py
+++ b/solution.py
@@ -38,7 +38,7 @@
     right,
     left,
     stats,
-    enc,
+    params,
     load_sem,
     rim_send,
     rim_recv,
@@ -46,7 +46,6 @@
     hid_recv,
     stat_send,
     stat_recv,
-    out_sem,
 ):
     frames, rows, width, c_in = video.shape
     past = cache_video.shape[0]
@@ -74,6 +73,8 @@
     for t in range(past):
         for r in range(out_rows):
             loads.append((cache_hidden.at[t, r], x2.at[1 + r, pl.ds(t * cols, cols)]))
+    for i, param in enumerate((gain_down, shift_down, gain_mix, shift_mix)):
+        loads.append((param, params.at[i]))
     copies = [pltpu.make_async_copy(s, d, load_sem.at[i]) for i, (s, d) in enumerate(loads)]
     for copy in copies:
         copy.start()
@@ -226,13 +227,14 @@
         copies[i].wait()
 
     center, inverse = wait_stats(0)
-    scale = inverse * gain_down[...]
-    shift = shift_down[...]
+    scale = inverse * params[0]
+    shift = params[1]
     for t in range(frames):
         for i in range(out_rows):
-            x2[1 + i, pl.ds((past + t) * cols, cols), :] = activate(
-                acc1[i, pl.ds(t * cols, cols), :], center, scale, shift
-            )
+            v = activate(acc1[i, pl.ds(t * cols, cols), :], center, scale, shift)
+            x2[1 + i, pl.ds((past + t) * cols, cols), :] = v
+            if t >= frames - past:
+                next_cache[t - frames + past, i] = v
 
         @pl.when(has_up)
         def _():
@@ -241,13 +243,6 @@
         @pl.when(has_down)
         def _():
             hid_copy(False, past + t).start()
-
-    outs = []
-    for t in range(past):
-        for r in range(out_rows):
-            src = x2.at[1 + r, pl.ds((total - past + t) * cols, cols)]
-            outs.append(pltpu.make_async_copy(src, next_cache.at[t, r], out_sem.at[len(outs)]))
-            outs[-1].start()
 
     everything = slice(0, c_out)
 
@@ -285,13 +280,11 @@
     send_stats(1, s, q)
 
     center, inverse = wait_stats(1)
-    scale = inverse * gain_mix[...]
-    shift = shift_mix[...]
+    scale = inverse * params[2]
+    shift = params[3]
     for t in range(frames):
         for i in range(out_rows):
-            enc[t, i] = activate(acc2[i, pl.ds(t * cols, cols), :], center, scale, shift)
-        outs.append(pltpu.make_async_copy(enc.at[t], encoded.at[t], out_sem.at[len(outs)]))
-        outs[-1].start()
+            encoded[t, i] = activate(acc2[i, pl.ds(t * cols, cols), :], center, scale, shift)
 
     @pl.when(has_up)
     def _():
@@ -309,16 +302,13 @@
         @pl.loop(1, n)
         def _(k):
             stat_copy(phase, me, lax.rem(me + k, n), k).wait_send()
-
-    for copy in outs:
-        copy.wait()
 
 
 def local(n, video, cache_video, cache_hidden, kernel_down, gain_down, shift_down, kernel_mix, gain_mix, shift_mix):
     frames, rows, width, c_in = video.shape
     past, out_rows, cols, c_out = cache_hidden.shape
     total = frames + past
-    hbm = pl.BlockSpec(memory_space=pl.ANY)
+    hbm = pl.BlockSpec(memory_space=pltpu.HBM)
     vmem = pl.BlockSpec(memory_space=pltpu.VMEM)
     row = lambda v: v.reshape(1, c_out)
     return pl.pallas_call(
@@ -327,8 +317,8 @@
             jax.ShapeDtypeStruct((frames, out_rows, cols, c_out), BF16),
             jax.ShapeDtypeStruct((past, out_rows, cols, c_out), BF16),
         ),
-        in_specs=[hbm, hbm, hbm, hbm, vmem, vmem, hbm, vmem, vmem],
-        out_specs=(hbm, hbm),
+        in_specs=[hbm] * 9,
+        out_specs=(vmem, vmem),
         scratch_shapes=[
             pltpu.VMEM((total, rows, width, c_in), BF16),
             pltpu.VMEM((total, width, c_in), BF16),
@@ -342,18 +332,17 @@
             pltpu.VMEM((out_rows, frames, cols + 8, c_out), F32),
             pltpu.VMEM((out_rows, frames, cols + 8, c_out), F32),
             pltpu.VMEM((2, n, 2, c_out), F32),
-            pltpu.VMEM((frames, out_rows, cols, c_out), BF16),
-            pltpu.SemaphoreType.DMA((total + 6 + past * out_rows,)),
+            pltpu.VMEM((4, 1, c_out), F32),
+            pltpu.SemaphoreType.DMA((total + 10 + past * out_rows,)),
             pltpu.SemaphoreType.DMA((total,)),
             pltpu.SemaphoreType.DMA((total,)),
             pltpu.SemaphoreType.DMA((2, total)),
             pltpu.SemaphoreType.DMA((2, total)),
             pltpu.SemaphoreType.DMA((2, n)),
             pltpu.SemaphoreType.DMA((2, n)),
-            pltpu.SemaphoreType.DMA((past * out_rows + frames,)),
         ],
         compiler_params=pltpu.CompilerParams(
-            collective_id=0, has_side_effects=True, vmem_limit_bytes=48 * 1024 * 1024
+            collective_id=0, has_side_effects=True, vmem_limit_bytes=67043328
         ),
     )(
         video,

time: 41.9 us -> 36.7 us (0.88)
  local copies, waits for them, and re-layouts: 8.9 us -> 3.54 us
    unnamed x18 -> x2, local copies, waits for them, and re-layouts: 8.9 us -> 3.54 us
where the time goes in v2:
time: 36.7 us; the launch traced here: 36.5 us
  Pallas kernels  32.3 us (88%)
  local copies, waits for them, and re-layouts  3.54 us (10%)
  between operations  0.64 us (2%)
    pallas_call x1, Pallas kernels, local(): pl.pallas_call(functools.partial(kernel, n), out_shape=(jax.ShapeDtypeStr...  32.3 us
    unnamed x2, local copies, waits for them, and re-layouts  3.54 us

profile of v2, /device:TPU:0, one launch (start us, length us, event | category | flops | bytes accessed | tf_op | source)
XLA Modules:
  0.0 36.5 jit_solution(6433443692896045476)
XLA Ops:
  0.6 32.3 %shard_map.104 = (bf16[4,2,128,256]{3,2,1,0:T(8,128)(2,1)}, bf16[2,2,128,256]{3,2,1,0:T(8,128)(2,1)}) custom-call(bf16[4,4,256,128]{3,2,1,0:T(8,128)(2,1)} %video.1, bf16[2,4,256,128]{3,2,1,0:T(8,128)(2,1)} %cache_video.1, bf16[2,2,128,256]{3,2,1,0:T(8,128)(2,1)} %cache_hidden.1, bf16[9,384,256]{2,1,0:T(8,128)(2,1)} %bitcast.7, f32[1,256]{1,0:T(1,128)} %bitcast.8, ...), custom_call_target="tpu_custom_call" | custom-call | tf_op jit(solution)/shard_map/pallas_call | solution.py:314
  33.0 1.9 %copy.13 = bf16[4,2,128,256]{3,2,1,0:T(8,128)(2,1)} copy(bf16[4,2,128,256]{3,2,1,0:T(8,128)(2,1)} %get-tuple-element.4) | data formatting | bytes 1048576
  34.8 1.7 %copy.14 = bf16[2,2,128,256]{3,2,1,0:T(8,128)(2,1)} copy(bf16[2,2,128,256]{3,2,1,0:T(8,128)(2,1)} %get-tuple-element.5) | data formatting | bytes 524288

commit v3 on v2

--- a/solution.py
+++ b/solution.py
@@ -39,6 +39,9 @@
     left,
     stats,
     params,
+    sent,
+    got,
+    means,
     load_sem,
     rim_send,
     rim_recv,
@@ -90,14 +93,16 @@
         )
 
     def hid_copy(up, t):
-        span = pl.ds(t * cols, cols)
+        side = 0 if up else 1
         if t < past:
             src = cache_hidden.at[t, 0 if up else out_rows - 1]
+            dst = x2.at[out_rows + 1 if up else 0, pl.ds(t * cols, cols)]
+        elif t < total:
+            src, dst = sent.at[side, t - past], got.at[side, t - past]
         else:
-            src = x2.at[1 if up else out_rows, span]
-        side = 0 if up else 1
+            src, dst = means.at[side], means.at[2 + side]
         return pltpu.make_async_remote_copy(
-            src_ref=src, dst_ref=x2.at[out_rows + 1 if up else 0, span],
+            src_ref=src, dst_ref=dst,
             send_sem=hid_send.at[side, t], recv_sem=hid_recv.at[side, t],
             device_id={"ha": me - 1 if up else me + 1}, device_id_type=MESH,
         )
@@ -148,23 +153,7 @@
     def as_frames(v):
         return v.reshape(frames, cols, c_out)
 
-    for i in range(out_rows):
-        pairs = [(a, 2 * i + b, b) for b in range(3) if 2 * i + b < rows for a in range(3)]
-        acc1[i] = taps(x1, both, w1, near, pairs)
-        right[i, :, pl.ds(0, cols), :] = as_frames(taps(x1, even, w1, far, pairs))
-
-    @pl.when(has_down)
-    def _():
-        for t in range(total):
-            rim_copy(t).wait_recv()
-            split(rim[t], t % rows, rows, t)
-
-    pairs = [(a, rows, 2) for a in range(3)]
-    last = out_rows - 1
-    acc1[last] += taps(x1, both, w1, near, pairs)
-    right[last, :, pl.ds(0, cols), :] += as_frames(taps(x1, even, w1, far, pairs))
-
-    def sums(parts, s, q, v):
+    def sums(s, q, v):
         v8 = v.reshape(cols // 8, 8, c_out)
         return s + jnp.sum(v8, axis=0), q + jnp.sum(v8 * v8, axis=0)
 
@@ -214,17 +203,65 @@
         v = (v - center) * scale + shift
         return (v / (1.0 + jnp.exp(-v))).astype(BF16)
 
-    s = q = jnp.zeros((8, c_out), F32)
-    for i in range(out_rows):
+    def down_row(i):
+        pairs = [(a, 2 * i + b, b) for b in range(3) if 2 * i + b < rows for a in range(3)]
+        acc1[i] = taps(x1, both, w1, near, pairs)
+        right[i, :, pl.ds(0, cols), :] = as_frames(taps(x1, even, w1, far, pairs))
+
+    def shifted_row(i, s, q):
+        row = jnp.zeros((8, c_out), F32)
         for t in range(frames):
             span = pl.ds(t * cols, cols)
             v = acc1[i, span, :] + right[i, t, pl.ds(1, cols), :]
             acc1[i, span, :] = v
-            s, q = sums(None, s, q, v)
+            row, q = sums(row, q, v)
+        return s + row, q, jnp.sum(row, axis=0, keepdims=True) / float(m)
+
+    def centre_row(side, i, mean):
+        means[side] = mean
+        for t in range(frames):
+            sent[side, t] = (acc1[i, pl.ds(t * cols, cols), :] - mean).astype(BF16)
+
+    s = q = jnp.zeros((8, c_out), F32)
+    last = out_rows - 1
+    for i in range(last):
+        down_row(i)
+        s, q, mean = shifted_row(i, s, q)
+        if i == 0:
+            centre_row(0, i, mean)
+
+            @pl.when(has_up)
+            def _():
+                for t in range(past, total + 1):
+                    hid_copy(True, t).start()
+
+    down_row(last)
+
+    @pl.when(has_down)
+    def _():
+        for t in range(total):
+            rim_copy(t).wait_recv()
+            split(rim[t], t % rows, rows, t)
+
+    pairs = [(a, rows, 2) for a in range(3)]
+    acc1[last] += taps(x1, both, w1, near, pairs)
+    right[last, :, pl.ds(0, cols), :] += as_frames(taps(x1, even, w1, far, pairs))
+    s, q, mean = shifted_row(last, s, q)
     send_stats(0, s, q)
+    centre_row(1, last, mean)
+
+    @pl.when(has_down)
+    def _():
+        for t in range(past, total + 1):
+            hid_copy(False, t).start()
 
     for i in range(total + 3, len(copies)):
         copies[i].wait()
+
+    everything = slice(0, c_out)
+
+    def mix(i, c, pairs):
+        return taps(x2, everything, w2, pl.ds(c * c_out, c_out), pairs)
 
     center, inverse = wait_stats(0)
     scale = inverse * params[0]
@@ -236,34 +273,29 @@
             if t >= frames - past:
                 next_cache[t - frames + past, i] = v
 
-        @pl.when(has_up)
-        def _():
-            hid_copy(True, past + t).start()
-
-        @pl.when(has_down)
-        def _():
-            hid_copy(False, past + t).start()
-
-    everything = slice(0, c_out)
-
-    def mix(i, c, pairs):
-        return taps(x2, everything, w2, pl.ds(c * c_out, c_out), pairs)
-
     for i in range(out_rows):
         pairs = [(a, i + b, b) for b in range(3) if 1 <= i + b <= out_rows for a in range(3)]
         left[i, :, pl.ds(8, cols), :] = as_frames(mix(i, 0, pairs))
         acc2[i] = mix(i, 1, pairs)
         right[i, :, pl.ds(0, cols), :] = as_frames(mix(i, 2, pairs))
 
+    def receive(up):
+        side = 0 if up else 1
+        for t in range(total + 1):
+            hid_copy(up, t).wait_recv()
+        offset = center - means[2 + side]
+        for t in range(frames):
+            x2[out_rows + 1 if up else 0, pl.ds((past + t) * cols, cols), :] = activate(
+                got[side, t].astype(F32), offset, scale, shift
+            )
+
     @pl.when(has_up)
     def _():
-        for t in range(total):
-            hid_copy(False, t).wait_recv()
+        receive(False)
 
     @pl.when(has_down)
     def _():
-        for t in range(total):
-            hid_copy(True, t).wait_recv()
+        receive(True)
 
     s = q = jnp.zeros((8, c_out), F32)
     for i in range(out_rows):
@@ -276,7 +308,7 @@
             span = pl.ds(t * cols, cols)
             v = acc2[i, span, :] + left[i, t, pl.ds(7, cols), :] + right[i, t, pl.ds(1, cols), :]
             acc2[i, span, :] = v
-            s, q = sums(None, s, q, v)
+            s, q = sums(s, q, v)
     send_stats(1, s, q)
 
     center, inverse = wait_stats(1)
@@ -290,11 +322,12 @@
     def _():
         for t in range(total):
             rim_copy(t).wait_send()
+        for t in range(total + 1):
             hid_copy(True, t).wait_send()
 
     @pl.when(has_down)
     def _():
-        for t in range(total):
+        for t in range(total + 1):
             hid_copy(False, t).wait_send()
 
     for phase in range(2):
@@ -333,11 +366,14 @@
             pltpu.VMEM((out_rows, frames, cols + 8, c_out), F32),
             pltpu.VMEM((2, n, 2, c_out), F32),
             pltpu.VMEM((4, 1, c_out), F32),
+            pltpu.VMEM((2, frames, cols, c_out), BF16),
+            pltpu.VMEM((2, frames, cols, c_out), BF16),
+            pltpu.VMEM((4, 1, c_out), F32),
             pltpu.SemaphoreType.DMA((total + 10 + past * out_rows,)),
             pltpu.SemaphoreType.DMA((total,)),
             pltpu.SemaphoreType.DMA((total,)),
-            pltpu.SemaphoreType.DMA((2, total)),
-            pltpu.SemaphoreType.DMA((2, total)),
+            pltpu.SemaphoreType.DMA((2, total + 1)),
+            pltpu.SemaphoreType.DMA((2, total + 1)),
             pltpu.SemaphoreType.DMA((2, n)),
             pltpu.SemaphoreType.DMA((2, n)),
         ],

time: 36.7 us -> 35.6 us (0.970)
  Pallas kernels: 32.3 us -> 31.2 us
    pallas_call x1, Pallas kernels: 32.3 us -> 31.2 us  [local(): pl.pallas_call(functools.partial(kernel, n), out_shape=(jax.ShapeDtypeStr...]
where the time goes in v3:
time: 35.6 us; the launch traced here: 35.4 us
  Pallas kernels  31.2 us (88%)
  local copies, waits for them, and re-layouts  3.54 us (10%)
  between operations  0.64 us (2%)
    pallas_call x1, Pallas kernels, local(): pl.pallas_call(functools.partial(kernel, n), out_shape=(jax.ShapeDtypeStr...  31.2 us
    unnamed x2, local copies, waits for them, and re-layouts  3.54 us

profile of v3, /device:TPU:0, one launch (start us, length us, event | category | flops | bytes accessed | tf_op | source)
XLA Modules:
  0.0 35.4 jit_solution(11942682888537562698)
XLA Ops:
  0.6 31.2 %shard_map.104 = (bf16[4,2,128,256]{3,2,1,0:T(8,128)(2,1)}, bf16[2,2,128,256]{3,2,1,0:T(8,128)(2,1)}) custom-call(bf16[4,4,256,128]{3,2,1,0:T(8,128)(2,1)} %video.1, bf16[2,4,256,128]{3,2,1,0:T(8,128)(2,1)} %cache_video.1, bf16[2,2,128,256]{3,2,1,0:T(8,128)(2,1)} %cache_hidden.1, bf16[9,384,256]{2,1,0:T(8,128)(2,1)} %bitcast.7, f32[1,256]{1,0:T(1,128)} %bitcast.8, ...), custom_call_target="tpu_custom_call" | custom-call | tf_op jit(solution)/shard_map/pallas_call | solution.py:347
  31.9 1.9 %copy.13 = bf16[4,2,128,256]{3,2,1,0:T(8,128)(2,1)} copy(bf16[4,2,128,256]{3,2,1,0:T(8,128)(2,1)} %get-tuple-element.4) | data formatting | bytes 1048576
  33.8 1.7 %copy.14 = bf16[2,2,128,256]{3,2,1,0:T(8,128)(2,1)} copy(bf16[2,2,128,256]{3,2,1,0:T(8,128)(2,1)} %get-tuple-element.5) | data formatting | bytes 524288

commit v4 on v3

--- a/solution.py
+++ b/solution.py
@@ -378,18 +378,23 @@
             pltpu.SemaphoreType.DMA((2, n)),
         ],
         compiler_params=pltpu.CompilerParams(
-            collective_id=0, has_side_effects=True, vmem_limit_bytes=67043328
+            collective_id=0, has_side_effects=True, vmem_limit_bytes=48 * 1024 * 1024
         ),
     )(
-        video,
-        cache_video,
-        cache_hidden,
-        kernel_down.reshape(9, 3 * c_in, c_out),
-        row(gain_down),
-        row(shift_down),
-        kernel_mix.reshape(9, 3 * c_out, c_out),
-        row(gain_mix),
-        row(shift_mix),
+        *(
+            pltpu.with_memory_space_constraint(v, pltpu.HBM)
+            for v in (
+                video,
+                cache_video,
+                cache_hidden,
+                kernel_down.reshape(9, 3 * c_in, c_out),
+                row(gain_down),
+                row(shift_down),
+                kernel_mix.reshape(9, 3 * c_out, c_out),
+                row(gain_mix),
+                row(shift_mix),
+            )
+        )
     )
 
 

time: 35.6 us -> 32.6 us (0.916)
  local copies, waits for them, and re-layouts: 3.54 us -> 1.5 us
  Pallas kernels: 31.2 us -> 30.3 us
    unnamed x2, local copies, waits for them, and re-layouts: 3.54 us -> 1.5 us
    pallas_call x1, Pallas kernels: 31.2 us -> 30.3 us  [local(): pl.pallas_call(functools.partial(kernel, n), out_shape=(jax.ShapeDtypeStr...]
where the time goes in v4:
time: 32.6 us; the launch traced here: 32.5 us
  Pallas kernels  30.3 us (93%)
  local copies, waits for them, and re-layouts  1.5 us (5%)
  between operations  0.64 us (2%)
    pallas_call x1, Pallas kernels, local(): pl.pallas_call(functools.partial(kernel, n), out_shape=(jax.ShapeDtypeStr...  30.3 us
    unnamed x2, local copies, waits for them, and re-layouts  1.5 us

profile of v4, /device:TPU:0, one launch (start us, length us, event | category | flops | bytes accessed | tf_op | source)
XLA Modules:
  0.0 32.5 jit_solution(16158780693141122675)
XLA Ops:
  0.6 30.3 %shard_map.104 = (bf16[4,2,128,256]{3,2,1,0:T(8,128)(2,1)S(1)}, bf16[2,2,128,256]{3,2,1,0:T(8,128)(2,1)S(1)}) custom-call(bf16[4,4,256,128]{3,2,1,0:T(8,128)(2,1)} %video.1, bf16[2,4,256,128]{3,2,1,0:T(8,128)(2,1)} %cache_video.1, bf16[2,2,128,256]{3,2,1,0:T(8,128)(2,1)} %cache_hidden.1, bf16[9,384,256]{2,1,0:T(8,128)(2,1)} %bitcast.7, f32[1,256]{1,0:T(1,128)} %bitcast.8, ...), custom_call_target="tpu_custom_call" | custom-call | tf_op jit(solution)/shard_map/pallas_call | solution.py:347
  31.0 0.8 %copy.13 = bf16[4,2,128,256]{3,2,1,0:T(8,128)(2,1)} copy(bf16[4,2,128,256]{3,2,1,0:T(8,128)(2,1)S(1)} %get-tuple-element.4) | data formatting | bytes 1048576
  31.8 0.7 %copy.14 = bf16[2,2,128,256]{3,2,1,0:T(8,128)(2,1)} copy(bf16[2,2,128,256]{3,2,1,0:T(8,128)(2,1)S(1)} %get-tuple-element.5) | data formatting | bytes 524288
